TPU v7x, 32 devices: a whole 2x2x4 slice. The times are simulated.
32 devices in a mesh: seq: 4 (over y, x), exp: 8 (over z, core).
Axes of the slice: x: 2, y: 2, z: 4, core: 2. Of those that a mesh axis runs over, the one named last changes fastest.
Arguments:
- queries: bfloat16 [4096, 3072], P(('seq', 'exp')), may hold values from -123 to 123
- keys: bfloat16 [4096, 512], P(('seq', 'exp')), may hold values from -6 to 6
- values: bfloat16 [4096, 512], P(('seq', 'exp')), may hold values from -9 to 9
- residual: bfloat16 [4096, 6144], P(('seq', 'exp')), may hold values from -51 to 51
- proj_weight: bfloat16 [3072, 6144], P('seq', 'exp'), may hold values from -0.109375 to 0.109375
- norm_gain: bfloat16 [6144], replicated, may hold values from 0.099609375 to 1.8984375
- router: bfloat16 [6144, 8], replicated, may hold values from -0.078125 to 0.078125
- expert_ids: int32 [4096, 2], P(('seq', 'exp')), may hold values from 0 to 7, all different within a row; in each aligned block of 128 rows (0 to 127, 128 to 255, ...) at most 33 rows name the same one
- u_gate_up: bfloat16 [8, 6144, 1024], P('exp'), may hold values from -0.078125 to 0.078125
- v_gate_up: bfloat16 [8, 2, 512, 8192], P('exp'), may hold values from -0.25 to 0.25
- u_down: bfloat16 [8, 8192, 512], P('exp'), may hold values from -0.0625 to 0.0625
- v_down: bfloat16 [8, 512, 6144], P('exp'), may hold values from -0.25 to 0.25
Outputs:
- layer_out: bfloat16 [4096, 6144], P(('seq', 'exp'))
Inputs may be any that keep to these rules, and one draw needn't show every extreme that they name: `expert_ids`: the two experts of a token differ. Among the tokens of one device no expert is named more than 33 times, and in some devices' tokens some expert is named exactly 33 times.
All inputs are finite; a program needn't handle non-finite values.
Results may differ from a plain program's by a relative error of at most 0.02.
Values may be sent and summed in bfloat16 or wider, within the bound.
A program may use at most 192 MiB of HBM per device.

v0:
```python
import jax
import jax.numpy as jnp
from jax import lax
from jax.sharding import PartitionSpec as P

D = 6144
HEADS = 24
KV_HEADS = 4
HEAD_DIM = 128
GROUP_HEADS = 3
EXPERTS = 8
RANK = 512
TOK_DEV = 128
CAP = 33


EPS = 1e-05


def swapped(x, axis, distance):
    return lax.ppermute(x, axis, [(i, i ^ 1 << distance) for i in range(lax.axis_size(axis))])


def passed_along(value, axis, steps):
    count = lax.axis_size(axis)
    pairs = [(source, (source + steps) % count) for source in range(count)]
    return lax.ppermute(value, axis, pairs)


def attend(current, query_rows, key_rows, value_rows, allowed):
    row_max, row_sum, weighted = current
    scores = jnp.einsum("qhd,kd->qhk", query_rows, key_rows, preferred_element_type=jnp.float32)
    scores = scores * HEAD_DIM ** (-0.5)
    if allowed is not None:
        scores = jnp.where(allowed[:, None, :], scores, -jnp.inf)
    new_max = jnp.maximum(row_max, jnp.max(scores, axis=-1))
    fading = jnp.exp(row_max - new_max)
    exp_terms = jnp.exp(scores - new_max[..., None])
    row_sum = row_sum * fading + jnp.sum(exp_terms, axis=-1)
    update = jnp.einsum(
        "qhk,kd->qhd",
        exp_terms.astype(jnp.bfloat16),
        value_rows,
        preferred_element_type=jnp.float32,
    )
    weighted = weighted * fading[..., None] + update
    return (new_max, row_sum, weighted)


def fresh_states(count_rows):
    query_step = min(512, count_rows)
    states = [
        (
            jnp.full((query_step, GROUP_HEADS), -1e30, jnp.float32),
            jnp.zeros((query_step, GROUP_HEADS), jnp.float32),
            jnp.zeros((query_step, GROUP_HEADS, HEAD_DIM), jnp.float32),
        )
    ]
    return states


def attend_all(states, query_rows, query_pos, key_rows, value_rows, key_pos, mode):
    current = states[0]
    if mode == "open":
        current = attend(current, query_rows, key_rows, value_rows, None)
    else:
        allowed = key_pos[None, :] <= query_pos[:, None]
        current = attend(current, query_rows, key_rows, value_rows, allowed)
    updated = [current]
    return updated


def pick_states(stacked, which):
    return [
        tuple((lax.dynamic_index_in_dim(member, which, 0, keepdims=False) for member in tile))
        for tile in stacked
    ]


def put_states(stacked, which, fresh):
    return [
        tuple(
            (
                lax.dynamic_update_index_in_dim(member, newer, which, 0)
                for member, newer in zip(tile, new_tile)
            )
        )
        for tile, new_tile in zip(stacked, fresh)
    ]


def finish(states):
    results = [weighted / row_sum[..., None] for row_max, row_sum, weighted in states]
    joined = results[0].astype(jnp.bfloat16)
    return joined.reshape(joined.shape[0], GROUP_HEADS * HEAD_DIM)


def per_device(
    queries,
    keys,
    values,
    residual,
    proj_weight,
    norm_gain,
    router,
    expert_ids,
    u_gate_up,
    v_gate_up,
    u_down,
    v_down,
):
    seq_count = lax.axis_size("seq")
    exp_count = lax.axis_size("exp")
    seq_index = lax.axis_index("seq")
    exp_index = lax.axis_index("exp")
    group_count = HEADS // GROUP_HEADS
    split_count = exp_count // group_count
    group_width = GROUP_HEADS * HEAD_DIM
    token_rows = TOK_DEV // split_count
    block_len = TOK_DEV * exp_count
    query_count = exp_count * token_rows
    per_kv = group_count // KV_HEADS
    half_index = exp_index // group_count
    query_send = queries.reshape(token_rows, exp_count, group_width)
    kv_shape = (TOK_DEV, split_count, KV_HEADS, per_kv, HEAD_DIM)
    key_send = jnp.broadcast_to(keys.reshape(TOK_DEV, 1, KV_HEADS, 1, HEAD_DIM), kv_shape).reshape(
        TOK_DEV, exp_count, HEAD_DIM
    )
    value_send = jnp.broadcast_to(
        values.reshape(TOK_DEV, 1, KV_HEADS, 1, HEAD_DIM), kv_shape
    ).reshape(TOK_DEV, exp_count, HEAD_DIM)
    query_got, key_got, value_got = (
        lax.all_to_all(query_send, "exp", split_axis=1, concat_axis=0, tiled=True),
        lax.all_to_all(key_send, "exp", split_axis=1, concat_axis=0, tiled=True),
        lax.all_to_all(value_send, "exp", split_axis=1, concat_axis=0, tiled=True),
    )
    query_local = query_got.reshape(query_count, GROUP_HEADS, HEAD_DIM)
    key_local = key_got.reshape(block_len, HEAD_DIM)
    value_local = value_got.reshape(block_len, HEAD_DIM)
    row_ids = jnp.arange(query_count, dtype=jnp.int32)
    in_block = row_ids // token_rows * TOK_DEV + row_ids % token_rows * split_count + half_index
    key_offsets = jnp.arange(block_len, dtype=jnp.int32)
    half_q = query_count // 2
    half_k = block_len // 2
    query_near = query_local[:half_q]
    query_far = query_local[half_q:]
    key_far = key_local[half_k:]
    value_far = value_local[half_k:]
    for bit_index in range(seq_count.bit_length() - 1):
        query_far, key_far, value_far = swapped((query_far, key_far, value_far), "seq", bit_index)
    mirror_index = seq_count - 1 - seq_index
    near_pos = seq_index * block_len + in_block[:half_q]
    far_pos = mirror_index * block_len + in_block[half_q:]
    query_pair = jnp.stack([query_near, query_far])
    pair_states = [
        tuple((jnp.stack([member, member]) for member in tile)) for tile in fresh_states(half_q)
    ]
    held_blocks = (key_local[:half_k], value_local[:half_k], key_far, value_far)
    for step_index in range(seq_count):
        if step_index + 1 < seq_count:
            arrived = passed_along(
                (held_blocks[0], held_blocks[1], held_blocks[2], held_blocks[3]), "seq", 1
            )
        source = (seq_index - step_index) % seq_count
        low_keys, low_values, high_keys, high_values = held_blocks
        if step_index == 0:
            low_pos = source * block_len + key_offsets[:half_k]
            high_pos = (seq_count - 1 - source) * block_len + half_k + key_offsets[:half_k]
            near_now = pick_states(pair_states, 0)
            near_now = attend_all(
                near_now, query_near, near_pos, low_keys, low_values, low_pos, "masked"
            )
            pair_states = put_states(pair_states, 0, near_now)
            far_now = pick_states(pair_states, 1)
            far_now = attend_all(
                far_now, query_far, far_pos, high_keys, high_values, high_pos, "masked"
            )
            pair_states = put_states(pair_states, 1, far_now)
        else:
            first_low = source <= seq_index
            first_slot = jnp.where(first_low, 0, 1).astype(jnp.int32)
            key_pick = jnp.where(first_low, low_keys, high_keys)
            value_pick = jnp.where(first_low, low_values, high_values)
            query_pick = lax.dynamic_index_in_dim(query_pair, first_slot, 0, keepdims=False)
            picked_states = attend_all(
                pick_states(pair_states, first_slot),
                query_pick,
                None,
                key_pick,
                value_pick,
                None,
                "open",
            )
            pair_states = put_states(pair_states, first_slot, picked_states)
        second_high = source >= seq_count - seq_index
        second_slot = jnp.where(second_high, 0, 1).astype(jnp.int32)
        key_pick = jnp.where(second_high, high_keys, low_keys)
        value_pick = jnp.where(second_high, high_values, low_values)
        query_pick = lax.dynamic_index_in_dim(query_pair, second_slot, 0, keepdims=False)
        picked_states = attend_all(
            pick_states(pair_states, second_slot),
            query_pick,
            None,
            key_pick,
            value_pick,
            None,
            "open",
        )
        pair_states = put_states(pair_states, second_slot, picked_states)
        if step_index + 1 < seq_count:
            held_blocks = arrived
    attended_near = finish(pick_states(pair_states, 0))
    attended_far = finish(pick_states(pair_states, 1))
    for bit_index in range(seq_count.bit_length() - 1):
        attended_far = swapped(attended_far, "seq", bit_index)
    attended = jnp.concatenate([attended_near, attended_far], axis=0)
    weight_rows = lax.all_gather(proj_weight, "seq", axis=0, tiled=True)
    column_count = weight_rows.shape[1]
    blank_sum = jnp.zeros((exp_count, token_rows, split_count, column_count), jnp.float32)
    carried = blank_sum
    shard_piece = lax.all_gather(attended, "exp", axis=0, tiled=True)
    start_row = jnp.int32(0)
    shard_total = shard_piece.shape[0] // query_count
    for shard_index in range(shard_total):
        device_id = start_row // query_count + shard_index
        group_id = device_id % group_count
        half_id = device_id // group_count
        weight_slice = lax.dynamic_slice_in_dim(weight_rows, group_id * group_width, group_width, 0)
        rows_now = shard_piece[shard_index * query_count : (shard_index + 1) * query_count]
        product = jnp.dot(rows_now, weight_slice, preferred_element_type=jnp.float32)
        product = product.reshape(exp_count, token_rows, 1, column_count)
        corner = (0, 0, half_id, 0)
        present = lax.dynamic_slice(carried, corner, (exp_count, token_rows, 1, column_count))
        carried = lax.dynamic_update_slice(carried, present + product, corner)
    projected = carried
    projected = projected.reshape(block_len, column_count)
    attn_block = projected.astype(jnp.bfloat16)
    attn_update = lax.all_to_all(attn_block, "exp", split_axis=0, concat_axis=1, tiled=True)
    stream = residual.astype(jnp.float32) + attn_update.astype(jnp.float32)
    mean_sq = jnp.mean(stream * stream, axis=-1, keepdims=True)
    normed = (stream * lax.rsqrt(mean_sq + EPS) * norm_gain.astype(jnp.float32)).astype(
        jnp.bfloat16
    )
    logits = jnp.dot(normed, router, preferred_element_type=jnp.float32)
    expert_range = jnp.arange(EXPERTS, dtype=jnp.int32)
    picked = (expert_ids[:, :, None] == expert_range[None, None, :]).astype(jnp.float32)
    chosen = jnp.sum(picked * logits[:, None, :], axis=-1)
    mix_first = jax.nn.sigmoid(chosen[:, 0] - chosen[:, 1])
    mix_second = jax.nn.sigmoid(chosen[:, 1] - chosen[:, 0])
    piece_count = exp_count // EXPERTS
    piece_width = D // piece_count
    flat_ids = expert_ids.reshape(TOK_DEV * 2)
    member = (flat_ids[:, None] == expert_range[None, :]).astype(jnp.int32)
    slot_of = jnp.sum((jnp.cumsum(member, axis=0) - 1) * member, axis=1)
    token_of = jnp.arange(TOK_DEV * 2, dtype=jnp.int32) // 2
    slot_range = jnp.arange(CAP, dtype=jnp.int32)
    filled = member[:, :, None] * (slot_of[:, None, None] == slot_range[None, None, :]).astype(
        jnp.int32
    )
    source_token = jnp.sum(filled * token_of[:, None, None], axis=0)
    occupied = jnp.sum(filled, axis=0)
    piece_range = jnp.arange(piece_count, dtype=jnp.int32)
    take_index = source_token[:, None, :] * piece_count + piece_range[None, :, None]
    normed_rows = normed.reshape(TOK_DEV * piece_count, piece_width)
    send_rows = jnp.take(normed_rows, take_index, axis=0) * occupied[:, None, :, None].astype(
        jnp.bfloat16
    )
    send_rows = send_rows.reshape(exp_count, CAP, piece_width)
    dispatched = lax.all_to_all(send_rows, "exp", split_axis=0, concat_axis=0, tiled=True)
    expert_rows = dispatched.reshape(exp_count * CAP, piece_width)
    rank_sum = jnp.dot(expert_rows, u_gate_up[0], preferred_element_type=jnp.float32)
    for bit_index in range(piece_count.bit_length() - 1):
        rank_sum = rank_sum + swapped(rank_sum.astype(jnp.bfloat16), "exp", bit_index).astype(
            rank_sum.dtype
        )
    rank_in = rank_sum.astype(jnp.bfloat16)
    gate_part = jnp.dot(rank_in[:, :RANK], v_gate_up[0, 0], preferred_element_type=jnp.float32)
    up_part = jnp.dot(rank_in[:, RANK:], v_gate_up[0, 1], preferred_element_type=jnp.float32)
    hidden = (jax.nn.silu(gate_part) * up_part).astype(jnp.bfloat16)
    down_sum = jnp.dot(hidden, u_down[0], preferred_element_type=jnp.float32)
    for bit_index in range(piece_count.bit_length() - 1):
        down_sum = down_sum + swapped(down_sum.astype(jnp.bfloat16), "exp", bit_index).astype(
            down_sum.dtype
        )
    expert_out = jnp.dot(
        down_sum.astype(jnp.bfloat16), v_down[0], preferred_element_type=jnp.float32
    ).astype(jnp.bfloat16)
    returned = lax.all_to_all(
        expert_out.reshape(exp_count, CAP, piece_width),
        "exp",
        split_axis=0,
        concat_axis=0,
        tiled=True,
    )
    returned_rows = returned.reshape(exp_count * CAP, piece_width)
    slot_pairs = slot_of.reshape(TOK_DEV, 2)
    fetch_index = (
        expert_ids[:, :, None] * piece_count + piece_range[None, None, :]
    ) * CAP + slot_pairs[:, :, None]
    fetched = jnp.take(returned_rows, fetch_index, axis=0).astype(jnp.float32)
    fetched = fetched.reshape(TOK_DEV, 2, D)
    mixture = mix_first[:, None] * fetched[:, 0] + mix_second[:, None] * fetched[:, 1]
    return (stream + mixture).astype(jnp.bfloat16)


def solution(mesh):
    in_specs = (
        P(("seq", "exp"), None),
        P(("seq", "exp"), None),
        P(("seq", "exp"), None),
        P(("seq", "exp"), None),
        P("seq", "exp"),
        P(),
        P(),
        P(("seq", "exp"), None),
        P("exp", None, None),
        P("exp", None, None, None),
        P("exp", None, None),
        P("exp", None, None),
    )
    out_specs = P(("seq", "exp"), None)
    return jax.shard_map(
        per_device, mesh=mesh, in_specs=in_specs, out_specs=out_specs, check_vma=False
    )
```

profile of v0, /device:TPU:0, one launch (start us, length us, event | category | flops | bytes accessed | tf_op | source)
XLA Modules:
  0.0 555.4 jit_solution(10118629330337509046)
XLA Ops:
  8.2 6.4 %all-to-all-start.1 = ((bf16[128,8,128]{2,0,1:T(8,128)(2,1)}), bf16[128,8,128]{2,0,1:T(8,128)(2,1)S(1)}, u32[]{:S(2)}, u32[]{:S(2)}) async-start(bf16[128,8,128]{2,0,1:T(8,128)(2,1)} %bitcast.3), calls=%async_computation.1 | async-start | bytes 524288 | tf_op jit(solution)/shard_map/all_to_all | solution.py:134
  14.6 0.9 copy_bitcast_fusion
  15.5 8.8 %all-to-all-done.1 = bf16[128,8,128]{2,0,1:T(8,128)(2,1)S(1)} async-done(((bf16[128,8,128]{2,0,1:T(8,128)(2,1)}), bf16[128,8,128]{2,0,1:T(8,128)(2,1)S(1)}, u32[]{:S(2)}, u32[]{:S(2)}) %all-to-all-start.1) | async-done | bytes 262176 | tf_op jit(solution)/shard_map/all_to_all | solution.py:134
  25.0 3.4 all-to-all-start.2
  28.4 2.3 copy.180
  30.7 7.3 %all-to-all-done.2 = bf16[128,8,128]{2,0,1:T(8,128)(2,1)S(1)} async-done(((bf16[128,8,128]{2,0,1:T(8,128)(2,1)}), bf16[128,8,128]{2,0,1:T(8,128)(2,1)S(1)}, u32[]{:S(2)}, u32[]{:S(2)}) %all-to-all-start.2) | async-done | bytes 262176 | tf_op jit(solution)/shard_map/all_to_all | solution.py:135
  38.0 3.5 all-to-all-start
  41.7 1.6 collective-permute-start.2
  44.1 4.0 collective-permute-done.2
  48.1 1.5 collective-permute-start.3
  50.3 1.5 collective-permute-start.5
  51.8 1.5 collective-permute-start.6
  53.8 1.5 collective-permute-start.7
  55.3 9.3 %collective-permute-done.5 = bf16[512,128]{1,0:T(8,128)(2,1)S(1)} collective-permute-done((bf16[512,128]{1,0:T(8,128)(2,1)S(1)}, bf16[512,128]{1,0:T(8,128)(2,1)S(1)}, u32[]{:S(2)}, u32[]{:S(2)}) %collective-permute-start.5) | collective-permute-done | bytes 131104 | tf_op jit(solution)/shard_map/ppermute | solution.py:21
  64.9 4.6 collective-permute-start.10
  69.5 2.7 collective-permute-done.7
  72.2 1.3 collective-permute-start.11
  73.5 4.3 collective-permute-done.9
  77.8 1.3 collective-permute-start.13
  79.4 3.6 collective-permute-done.10
  83.3 2.5 collective-permute-done.12
  86.1 2.5 collective-permute-done.11
  88.9 2.5 collective-permute-done.13
  92.8 0.9 copy.188
  93.7 1.0 collective-permute-start
  97.5 11.0 %collective-permute-done = bf16[512,3,128]{2,0,1:T(8,128)(2,1)} collective-permute-done((bf16[512,3,128]{2,0,1:T(8,128)(2,1)}, bf16[512,3,128]{2,0,1:T(8,128)(2,1)}, u32[]{:S(2)}, u32[]{:S(2)}) %collective-permute-start) | collective-permute-done | bytes 393248 | tf_op jit(solution)/shard_map/ppermute | solution.py:21
  108.5 1.5 collective-permute-start.1
  110.4 2.8 fusion.149
  113.3 15.1 %collective-permute-done.1 = bf16[512,3,128]{2,0,1:T(8,128)(2,1)S(1)} collective-permute-done((bf16[512,3,128]{2,0,1:T(8,128)(2,1)}, bf16[512,3,128]{2,0,1:T(8,128)(2,1)S(1)}, u32[]{:S(2)}, u32[]{:S(2)}) %collective-permute-start.1) | collective-permute-done | bytes 393248 | tf_op jit(solution)/shard_map/ppermute | solution.py:21
  131.1 0.9 fusion.155
  145.6 1.3 collective-permute-start.18
  146.9 7.8 %collective-permute-done.18 = bf16[512,384]{0,1:T(8,128)(2,1)S(1)} collective-permute-done((bf16[512,384]{0,1:T(8,128)(2,1)S(1)}, bf16[512,384]{0,1:T(8,128)(2,1)S(1)}, u32[]{:S(2)}, u32[]{:S(2)}) %collective-permute-start.18) | collective-permute-done | bytes 393248 | tf_op jit(solution)/shard_map/ppermute | solution.py:21
  155.6 7.3 %collective-permute-done.19 = bf16[512,384]{0,1:T(8,128)(2,1)S(1)} collective-permute-done((bf16[512,384]{0,1:T(8,128)(2,1)S(1)}, bf16[512,384]{0,1:T(8,128)(2,1)S(1)}, u32[]{:S(2)}, u32[]{:S(2)}) %collective-permute-start.19) | collective-permute-done | bytes 393248 | tf_op jit(solution)/shard_map/ppermute | solution.py:21
  163.0 1.0 pad_maximum_fusion.1
  164.0 63.2 %all-gather.3.cloned.1.call-done = bf16[8192,384]{0,1:T(8,128)(2,1)} async-done(((bf16[1024,384]{0,1:T(8,128)(2,1)}), bf16[8192,384]{0,1:T(8,128)(2,1)}) %all-gather.3.cloned.1.call-update) | async-done | bytes 6291472 | tf_op jit(solution)/shard_map/all_gather | solution.py:221
  227.2 2.5 fusion.167
  229.7 2.5 fusion.169
  232.2 2.1 fusion.171
  234.3 1.0 fusion.173
  235.3 1.3 fusion.175
  236.6 1.0 fusion.177
  237.6 1.0 fusion.179
  238.6 3.8 add_convert_fusion
  242.4 3.7 all-to-all-start.3
  247.6 1.2 multiply_reduce_fusion.8
  249.1 34.8 %all-to-all-done.3 = bf16[8,128,768]{2,1,0:T(8,128)(2,1)S(1)} async-done(((bf16[8,128,768]{2,1,0:T(8,128)(2,1)}), bf16[8,128,768]{2,1,0:T(8,128)(2,1)S(1)}, u32[]{:S(2)}, u32[]{:S(2)}) %all-to-all-start.3) | async-done | bytes 1572896 | tf_op jit(solution)/shard_map/all_to_all | solution.py:238
  284.5 1.3 copy-done.4
  286.9 5.0 gather_fusion
  291.9 4.9 gather.13
  296.9 2.5 select_multiply_fusion
  299.4 92.1 %all_to_all.68 = bf16[8,33,6144]{2,1,0:T(8,128)(2,1)} all-to-all(bf16[8,33,6144]{2,1,0:T(8,128)(2,1)S(1)} %select_multiply_fusion), channel_id=1, replica_groups=mesh['seq'=4,'exp'=8] {'exp'}, dimensions={0} | all-to-all | bytes 6488064 | tf_op jit(solution)/shard_map/all_to_all | solution.py:269
  391.5 5.0 reshape.493
  396.5 9.1 %fusion.80 = bf16[264,1024]{1,0:T(8,128)(2,1)S(1)} fusion(bf16[264,6144]{1,0:T(8,128)(2,1)} %reshape.493, bf16[1,6144,1024]{2,1,0:T(8,128)(2,1)} %param.20), kind=kOutput, calls=%fused_computation.117 | convolution fusion | flops 3322159104 | bytes 16367616 | tf_op jit(solution)/shard_map/dot_general | solution.py:271
  405.6 9.1 %fusion.6 = f32[264,8192]{1,0:T(8,128)} fusion(bf16[1,2,512,8192]{3,2,1,0:T(8,128)(2,1)} %param.21, bf16[264,1024]{1,0:T(8,128)(2,1)S(1)} %fusion.80), kind=kOutput, calls=%fused_computation.9 | convolution fusion | flops 2214592512 | bytes 17309696 | tf_op jit(solution)/shard_map/dot_general | solution.py:277
  414.8 11.2 %fusion.158 = bf16[264,512]{1,0:T(8,128)(2,1)S(1)} fusion(bf16[1,8192,512]{2,1,0:T(8,128)(2,1)} %param.22, f32[264,8192]{1,0:T(8,128)} %fusion.6, bf16[1,2,512,8192]{3,2,1,0:T(8,128)(2,1)} %param.21, bf16[264,1024]{1,0:T(8,128)(2,1)S(1)} %fusion.80), kind=kOutput, calls=%fused_computation.143 | convolution fusion | flops 4442296320 | bytes 25968640 | tf_op jit(solution)/shard_map/dot_general | solution.py:280
  425.9 6.4 %convolution_convert_fusion = bf16[264,6144]{1,0:T(8,128)(2,1)} fusion(bf16[264,512]{1,0:T(8,128)(2,1)S(1)} %fusion.158, bf16[1,512,6144]{2,1,0:T(8,128)(2,1)} %param.23), kind=kOutput, calls=%fused_computation.13 | convolution fusion | flops 1662566400 | bytes 9805824 | tf_op jit(solution)/shard_map/dot_general | solution.py:285
  432.3 4.9 reshape.494
  437.2 4.8 all-to-all-start.5
  443.1 87.3 %all-to-all-done.5 = bf16[8,33,6144]{2,1,0:T(8,128)(2,1)} async-done(((bf16[8,33,6144]{2,1,0:T(8,128)(2,1)}), bf16[8,33,6144]{2,1,0:T(8,128)(2,1)}, u32[]{:S(2)}, u32[]{:S(2)}) %all-to-all-start.5) | async-done | bytes 3244064 | tf_op jit(solution)/shard_map/all_to_all | solution.py:288
  530.4 3.3 reshape.495
  533.7 4.1 gather_fusion.1
  537.8 5.9 %gather.15 = bf16[128,2,6144]{2,1,0:T(2,128)(2,1)S(1)} reshape(bf16[256,6144]{1,0:T(8,128)(2,1)} %gather_fusion.1) | data formatting | bytes 6291456 | tf_op jit(solution)/shard_map/jit(_take)/gather | solution.py:300
  543.8 2.0 fusion.19
  546.1 2.3 fusion.17
  (165 shorter events, 31.9 us)
Async XLA Ops:
  6.5 0.9 copy-start
  8.2 16.1 %all-to-all-start.1 = ((bf16[128,8,128]{2,0,1:T(8,128)(2,1)}), bf16[128,8,128]{2,0,1:T(8,128)(2,1)S(1)}, u32[]{:S(2)}, u32[]{:S(2)}) async-start(bf16[128,8,128]{2,0,1:T(8,128)(2,1)} %bitcast.3), calls=%async_computation.1 | async-start | bytes 524288 | tf_op jit(solution)/shard_map/all_to_all | solution.py:134
  25.0 13.1 %all-to-all-start.2 = ((bf16[128,8,128]{2,0,1:T(8,128)(2,1)}), bf16[128,8,128]{2,0,1:T(8,128)(2,1)S(1)}, u32[]{:S(2)}, u32[]{:S(2)}) async-start(bf16[128,8,128]{2,0,1:T(8,128)(2,1)} %bitcast.8), calls=%async_computation.2 | async-start | bytes 524288 | tf_op jit(solution)/shard_map/all_to_all | solution.py:135
  38.0 54.2 %all-to-all-start = ((bf16[128,8,384]{0,2,1:T(8,128)(2,1)}), bf16[128,8,384]{0,2,1:T(8,128)(2,1)S(1)}, u32[]{:S(2)}, u32[]{:S(2)}) async-start(bf16[128,8,384]{0,2,1:T(8,128)(2,1)} %bitcast), calls=%async_computation | async-start | bytes 1572864 | tf_op jit(solution)/shard_map/all_to_all | solution.py:133
  41.6 122.4 %all-gather.5.cloned.1.call-start = ((), (), s32[]{:S(2)}) async-start(), calls=%async_computation.7 | async-start | bytes 5898240 | tf_op jit(solution)/shard_map/all_gather | solution.py:217
  41.7 6.4 %collective-permute-start.2 = (bf16[512,128]{1,0:T(8,128)(2,1)S(1)}, bf16[512,128]{1,0:T(8,128)(2,1)S(1)}, u32[]{:S(2)}, u32[]{:S(2)}) collective-permute-start(bf16[512,128]{1,0:T(8,128)(2,1)S(1)} %bitcast.406), channel_id=1, source_target_pairs={{0,8},{8,0},{16,24},{24,16},{1,9},{9,1},{17,25},{25,17},{2,10},{10... | collective-permute-start | bytes 393224 | tf_op jit(solution)/shard_map/ppermute | solution.py:21
  43.3 26.2 %copy-start.9 = (bf16[4,128,1,128]{3,1,0,2:T(8,128)(2,1)}, bf16[4,128,1,128]{3,1,0,2:T(8,128)(2,1)S(1)}, u32[]{:S(2)}) copy-start(bf16[4,128,1,128]{3,1,0,2:T(8,128)(2,1)S(1)} %get-tuple-element.29) | copy-start | bytes 393220
  43.3 7.0 %collective-permute-start.4 = (bf16[512,128]{1,0:T(8,128)(2,1)S(1)}, bf16[512,128]{1,0:T(8,128)(2,1)S(1)}, u32[]{:S(2)}, u32[]{:S(2)}) collective-permute-start(bf16[512,128]{1,0:T(8,128)(2,1)S(1)} %bitcast.407), channel_id=1, source_target_pairs={{0,8},{8,0},{16,24},{24,16},{1,9},{9,1},{17,25},{25,17},{2,10},{10... | collective-permute-start | bytes 393224 | tf_op jit(solution)/shard_map/ppermute | solution.py:21
  43.9 183.3 %all-gather.3.cloned.1.call-start = ((), (), s32[]{:S(2)}) async-start(), calls=%async_computation.6 | async-start | bytes 7077888 | tf_op jit(solution)/shard_map/all_gather | solution.py:221
  48.1 5.7 %collective-permute-start.3 = (bf16[512,128]{1,0:T(8,128)(2,1)S(1)}, bf16[512,128]{1,0:T(8,128)(2,1)S(1)}, u32[]{:S(2)}, u32[]{:S(2)}) collective-permute-start(bf16[512,128]{1,0:T(8,128)(2,1)S(1)} %collective-permute-done.2), channel_id=1, source_target_pairs={{0,16},{8,24},{16,0},{24,8},{1,17},{9,25},{17,1},{25,9},{2,18},{10... | collective-permute-start | bytes 393224 | tf_op jit(solution)/shard_map/ppermute | solution.py:21
  50.3 14.3 %collective-permute-start.5 = (bf16[512,128]{1,0:T(8,128)(2,1)S(1)}, bf16[512,128]{1,0:T(8,128)(2,1)S(1)}, u32[]{:S(2)}, u32[]{:S(2)}) collective-permute-start(bf16[512,128]{1,0:T(8,128)(2,1)S(1)} %collective-permute-done.4), channel_id=1, source_target_pairs={{0,16},{8,24},{16,0},{24,8},{1,17},{9,25},{17,1},{25,9},{2,18},{10... | collective-permute-start | bytes 393224 | tf_op jit(solution)/shard_map/ppermute | solution.py:21
  51.8 13.0 %collective-permute-start.6 = (bf16[512,128]{1,0:T(8,128)(2,1)S(1)}, bf16[512,128]{1,0:T(8,128)(2,1)S(1)}, u32[]{:S(2)}, u32[]{:S(2)}) collective-permute-start(bf16[512,128]{1,0:T(8,128)(2,1)S(1)} %bitcast.398), channel_id=1, source_target_pairs={{0,8},{8,16},{16,24},{24,0},{1,9},{9,17},{17,25},{25,1},{2,10},{10... | collective-permute-start | bytes 393224 | tf_op jit(solution)/shard_map/ppermute | solution.py:27
  53.3 16.1 %collective-permute-start.8 = (bf16[512,128]{1,0:T(8,128)(2,1)S(1)}, bf16[512,128]{1,0:T(8,128)(2,1)S(1)}, u32[]{:S(2)}, u32[]{:S(2)}) collective-permute-start(bf16[512,128]{1,0:T(8,128)(2,1)S(1)} %bitcast.403), channel_id=1, source_target_pairs={{0,8},{8,16},{16,24},{24,0},{1,9},{9,17},{17,25},{25,1},{2,10},{10... | collective-permute-start | bytes 393224 | tf_op jit(solution)/shard_map/ppermute | solution.py:27
  53.8 18.4 %collective-permute-start.7 = (bf16[512,128]{1,0:T(8,128)(2,1)S(1)}, bf16[512,128]{1,0:T(8,128)(2,1)S(1)}, u32[]{:S(2)}, u32[]{:S(2)}) collective-permute-start(bf16[512,128]{1,0:T(8,128)(2,1)S(1)} %collective-permute-done.3), channel_id=1, source_target_pairs={{0,8},{8,16},{16,24},{24,0},{1,9},{9,17},{17,25},{25,1},{2,10},{10... | collective-permute-start | bytes 393224 | tf_op jit(solution)/shard_map/ppermute | solution.py:27
  64.6 21.5 %copy-start.11 = (bf16[512,128]{1,0:T(8,128)(2,1)}, bf16[512,128]{1,0:T(8,128)(2,1)S(1)}, u32[]{:S(2)}) copy-start(bf16[512,128]{1,0:T(8,128)(2,1)S(1)} %collective-permute-done.5) | copy-start | bytes 393220
  64.6 13.2 %collective-permute-start.9 = (bf16[512,128]{1,0:T(8,128)(2,1)S(1)}, bf16[512,128]{1,0:T(8,128)(2,1)S(1)}, u32[]{:S(2)}, u32[]{:S(2)}) collective-permute-start(bf16[512,128]{1,0:T(8,128)(2,1)S(1)} %collective-permute-done.5), channel_id=1, source_target_pairs={{0,8},{8,16},{16,24},{24,0},{1,9},{9,17},{17,25},{25,1},{2,10},{10... | collective-permute-start | bytes 393224 | tf_op jit(solution)/shard_map/ppermute | solution.py:27
  64.9 18.1 %collective-permute-start.10 = (bf16[512,128]{1,0:T(8,128)(2,1)S(1)}, bf16[512,128]{1,0:T(8,128)(2,1)S(1)}, u32[]{:S(2)}, u32[]{:S(2)}) collective-permute-start(bf16[512,128]{1,0:T(8,128)(2,1)S(1)} %collective-permute-done.6), channel_id=1, source_target_pairs={{0,8},{8,16},{16,24},{24,0},{1,9},{9,17},{17,25},{25,1},{2,10},{10... | collective-permute-start | bytes 393224 | tf_op jit(solution)/shard_map/ppermute | solution.py:27
  69.4 16.4 %collective-permute-start.12 = (bf16[512,128]{1,0:T(8,128)(2,1)S(1)}, bf16[512,128]{1,0:T(8,128)(2,1)S(1)}, u32[]{:S(2)}, u32[]{:S(2)}) collective-permute-start(bf16[512,128]{1,0:T(8,128)(2,1)S(1)} %collective-permute-done.8), channel_id=1, source_target_pairs={{0,8},{8,16},{16,24},{24,0},{1,9},{9,17},{17,25},{25,1},{2,10},{10... | collective-permute-start | bytes 393224 | tf_op jit(solution)/shard_map/ppermute | solution.py:27
  72.2 16.4 %collective-permute-start.11 = (bf16[512,128]{1,0:T(8,128)(2,1)S(1)}, bf16[512,128]{1,0:T(8,128)(2,1)S(1)}, u32[]{:S(2)}, u32[]{:S(2)}) collective-permute-start(bf16[512,128]{1,0:T(8,128)(2,1)S(1)} %collective-permute-done.7), channel_id=1, source_target_pairs={{0,8},{8,16},{16,24},{24,0},{1,9},{9,17},{17,25},{25,1},{2,10},{10... | collective-permute-start | bytes 393224 | tf_op jit(solution)/shard_map/ppermute | solution.py:27
  77.8 13.6 %collective-permute-start.13 = (bf16[512,128]{1,0:T(8,128)(2,1)S(1)}, bf16[512,128]{1,0:T(8,128)(2,1)S(1)}, u32[]{:S(2)}, u32[]{:S(2)}) collective-permute-start(bf16[512,128]{1,0:T(8,128)(2,1)S(1)} %collective-permute-done.9), channel_id=1, source_target_pairs={{0,8},{8,16},{16,24},{24,0},{1,9},{9,17},{17,25},{25,1},{2,10},{10... | collective-permute-start | bytes 393224 | tf_op jit(solution)/shard_map/ppermute | solution.py:27
  83.0 57.6 %collective-permute-start.14 = (bf16[512,128]{1,0:T(8,128)(2,1)S(1)}, bf16[512,128]{1,0:T(8,128)(2,1)S(1)}, u32[]{:S(2)}, u32[]{:S(2)}) collective-permute-start(bf16[512,128]{1,0:T(8,128)(2,1)S(1)} %collective-permute-done.10), channel_id=1, source_target_pairs={{0,8},{8,16},{16,24},{24,0},{1,9},{9,17},{17,25},{25,1},{2,10},{10... | collective-permute-start | bytes 393224 | tf_op jit(solution)/shard_map/ppermute | solution.py:27
  85.8 56.3 %collective-permute-start.16 = (bf16[512,128]{1,0:T(8,128)(2,1)S(1)}, bf16[512,128]{1,0:T(8,128)(2,1)S(1)}, u32[]{:S(2)}, u32[]{:S(2)}) collective-permute-start(bf16[512,128]{1,0:T(8,128)(2,1)S(1)} %collective-permute-done.12), channel_id=1, source_target_pairs={{0,8},{8,16},{16,24},{24,0},{1,9},{9,17},{17,25},{25,1},{2,10},{10... | collective-permute-start | bytes 393224 | tf_op jit(solution)/shard_map/ppermute | solution.py:27
  88.6 52.0 %collective-permute-start.15 = (bf16[512,128]{1,0:T(8,128)(2,1)S(1)}, bf16[512,128]{1,0:T(8,128)(2,1)S(1)}, u32[]{:S(2)}, u32[]{:S(2)}) collective-permute-start(bf16[512,128]{1,0:T(8,128)(2,1)S(1)} %collective-permute-done.11), channel_id=1, source_target_pairs={{0,8},{8,16},{16,24},{24,0},{1,9},{9,17},{17,25},{25,1},{2,10},{10... | collective-permute-start | bytes 393224 | tf_op jit(solution)/shard_map/ppermute | solution.py:27
  91.4 50.7 %collective-permute-start.17 = (bf16[512,128]{1,0:T(8,128)(2,1)S(1)}, bf16[512,128]{1,0:T(8,128)(2,1)S(1)}, u32[]{:S(2)}, u32[]{:S(2)}) collective-permute-start(bf16[512,128]{1,0:T(8,128)(2,1)S(1)} %collective-permute-done.13), channel_id=1, source_target_pairs={{0,8},{8,16},{16,24},{24,0},{1,9},{9,17},{17,25},{25,1},{2,10},{10... | collective-permute-start | bytes 393224 | tf_op jit(solution)/shard_map/ppermute | solution.py:27
  93.7 14.8 %collective-permute-start = (bf16[512,3,128]{2,0,1:T(8,128)(2,1)}, bf16[512,3,128]{2,0,1:T(8,128)(2,1)}, u32[]{:S(2)}, u32[]{:S(2)}) collective-permute-start(bf16[512,3,128]{2,0,1:T(8,128)(2,1)} %copy.188), channel_id=1, source_target_pairs={{0,8},{8,0},{16,24},{24,16},{1,9},{9,1},{17,25},{25,17},{2,10},{10... | collective-permute-start | bytes 1179656 | tf_op jit(solution)/shard_map/ppermute | solution.py:21
  95.9 1.6 copy-start.6
  96.5 12.0 %copy-start.14 = (f32[512,3]{0,1:T(4,128)}, f32[512,3]{0,1:T(4,128)S(1)}, u32[]{:S(2)}) copy-start(f32[512,3]{0,1:T(4,128)S(1)} %get-tuple-element.47) | copy-start | bytes 18436
  108.5 19.9 %collective-permute-start.1 = (bf16[512,3,128]{2,0,1:T(8,128)(2,1)}, bf16[512,3,128]{2,0,1:T(8,128)(2,1)S(1)}, u32[]{:S(2)}, u32[]{:S(2)}) collective-permute-start(bf16[512,3,128]{2,0,1:T(8,128)(2,1)} %collective-permute-done), channel_id=1, source_target_pairs={{0,16},{8,24},{16,0},{24,8},{1,17},{9,25},{17,1},{25,9},{2,18},{10... | collective-permute-start | bytes 1179656 | tf_op jit(solution)/shard_map/ppermute | solution.py:21
  129.8 1.3 copy-start.12
  131.1 1.1 copy-start.10
  145.6 9.1 %collective-permute-start.18 = (bf16[512,384]{0,1:T(8,128)(2,1)S(1)}, bf16[512,384]{0,1:T(8,128)(2,1)S(1)}, u32[]{:S(2)}, u32[]{:S(2)}) collective-permute-start(bf16[512,384]{0,1:T(8,128)(2,1)S(1)} %fusion.181), channel_id=1, source_target_pairs={{0,8},{8,0},{16,24},{24,16},{1,9},{9,1},{17,25},{25,17},{2,10},{10... | collective-permute-start | bytes 1179656 | tf_op jit(solution)/shard_map/ppermute | solution.py:21
  154.8 8.2 %collective-permute-start.19 = (bf16[512,384]{0,1:T(8,128)(2,1)S(1)}, bf16[512,384]{0,1:T(8,128)(2,1)S(1)}, u32[]{:S(2)}, u32[]{:S(2)}) collective-permute-start(bf16[512,384]{0,1:T(8,128)(2,1)S(1)} %collective-permute-done.18), channel_id=1, source_target_pairs={{0,16},{8,24},{16,0},{24,8},{1,17},{9,25},{17,1},{25,9},{2,18},{10... | collective-permute-start | bytes 1179656 | tf_op jit(solution)/shard_map/ppermute | solution.py:21
  227.2 5.0 copy-start.7
  229.7 4.6 copy-start.8
  242.4 3.7 copy-start.16
  242.4 4.1 copy-start.15
  242.4 41.4 %all-to-all-start.3 = ((bf16[8,128,768]{2,1,0:T(8,128)(2,1)}), bf16[8,128,768]{2,1,0:T(8,128)(2,1)S(1)}, u32[]{:S(2)}, u32[]{:S(2)}) async-start(bf16[8,128,768]{2,1,0:T(8,128)(2,1)} %bitcast.89), calls=%async_computation.3 | async-start | bytes 3145728 | tf_op jit(solution)/shard_map/all_to_all | solution.py:238
  284.2 1.7 copy-start.4
  284.5 1.8 copy-start.2
  437.2 5.3 copy-start.13
  437.2 93.2 %all-to-all-start.5 = ((bf16[8,33,6144]{2,1,0:T(8,128)(2,1)}), bf16[8,33,6144]{2,1,0:T(8,128)(2,1)}, u32[]{:S(2)}, u32[]{:S(2)}) async-start(bf16[8,33,6144]{2,1,0:T(8,128)(2,1)} %reshape.494), calls=%async_computation.5 | async-start | bytes 7864320 | tf_op jit(solution)/shard_map/all_to_all | solution.py:288
  543.7 2.1 copy-start.3
  543.7 2.3 copy-start.5
  546.1 2.3 copy-start.1
Sparse Core Ops, SparseCore 0:
  44.3 99.9 all-gather.4
  164.1 63.0 all-gather.2
where the time goes:
time: 559 us; the launch traced here: 555 us
  waiting for transfers between devices  275 us (49%)
  blocking collectives  92.1 us (16%)
  matrix products  66.2 us (12%)
  local copies, waits for them, and re-layouts  45.2 us (8%)
  starting transfers between devices  44.3 us (8%)
  other arithmetic  18.2 us (3%)
  between operations  14.6 us (3%)
    all_to_all x1, blocking collectives, per_device(): lax.all_to_all(send_rows, 'exp', split_axis=0, concat_axis=0, tiled=True)  92.1 us
    all_to_all x1, waiting for transfers between devices, per_device(): lax.all_to_all(expert_out.reshape(exp_count, CAP, piece_width), 'exp', sp...  87.3 us
    all_gather x1, waiting for transfers between devices, per_device(): shard_piece = lax.all_gather(attended, 'exp', axis=0, tiled=True)  63.2 us
    ppermute x8, waiting for transfers between devices, swapped(): lax.ppermute(x, axis, [(i, i ^ 1 << distance) for i in range(lax.axis_siz...  55.4 us
    all_to_all x1, waiting for transfers between devices, per_device(): lax.all_to_all(attn_block, 'exp', split_axis=0, concat_axis=1, tiled=True)  34.8 us
    ppermute x12, waiting for transfers between devices, passed_along(): return lax.ppermute(value, axis, pairs)  18.1 us
    dot_general x8, matrix products, per_device(): jnp.dot(rows_now, weight_slice, preferred_element_type=jnp.float32)  15.1 us
    ppermute x12, starting transfers between devices, passed_along(): return lax.ppermute(value, axis, pairs)  12.6 us
  transfers between devices with their start and end apart: 27, of which 18 were waited for; matrix products, arithmetic and copies ran while one was open for 6% of the time, Pallas kernels for 0%

commit v1 on v0

v1 whole, which is shorter than its diff:
```python
import functools

import jax
import jax.numpy as jnp
from jax import lax
from jax.experimental import pallas as pl
from jax.experimental.pallas import tpu as pltpu
from jax.sharding import PartitionSpec as P

D = 6144
HEADS = 24
KV_HEADS = 4
HEAD_DIM = 128
EXPERTS = 8
RANK = 512
TOK_DEV = 128
CAP = 33


EPS = 1e-05
LOG2_E = 1.4426950408889634


def swapped(x, axis, distance):
    return lax.ppermute(x, axis, [(i, i ^ 1 << distance) for i in range(lax.axis_size(axis))])


def attention_kernel(heads, parts, q_ref, kv_ref, out_ref):
    block = pl.program_id(0)
    column = lax.axis_index("exp")
    columns = kv_ref.shape[0]
    span = columns // parts
    chunk = span * TOK_DEV
    rows = heads * TOK_DEV
    query = jnp.concatenate(
        [q_ref[:, h * HEAD_DIM : (h + 1) * HEAD_DIM] for h in range(heads)], axis=0
    )

    def step(index, carried, masked):
        row_max, row_sum, weighted = carried
        held = kv_ref[pl.ds((index % parts) * span, span), index // parts]
        held = held.reshape(chunk, 2 * HEAD_DIM)
        scores = lax.dot_general(
            query, held[:, :HEAD_DIM], (((1,), (1,)), ((), ())), preferred_element_type=jnp.float32
        ) * (HEAD_DIM ** (-0.5) * LOG2_E)
        if masked:
            offset = (column % span) * TOK_DEV
            own = lax.broadcasted_iota(jnp.int32, (rows, chunk), 0) % TOK_DEV + offset
            other = lax.broadcasted_iota(jnp.int32, (rows, chunk), 1)
            scores = jnp.where(other <= own, scores, -jnp.inf)
        new_max = jnp.maximum(row_max, jnp.max(scores, axis=-1, keepdims=True))
        fading = jnp.exp2(row_max - new_max)
        terms = jnp.exp2(scores - new_max)
        row_sum = row_sum * fading + jnp.sum(terms, axis=-1, keepdims=True)
        update = jnp.dot(
            terms.astype(jnp.bfloat16), held[:, HEAD_DIM:], preferred_element_type=jnp.float32
        )
        return new_max, row_sum, weighted * fading + update

    carried = (
        jnp.full((rows, 1), -1e30, jnp.float32),
        jnp.zeros((rows, 1), jnp.float32),
        jnp.zeros((rows, HEAD_DIM), jnp.float32),
    )
    last = block * parts + column // span
    carried = lax.fori_loop(0, last, lambda index, now: step(index, now, False), carried)
    row_max, row_sum, weighted = step(last, carried, True)
    result = (weighted / row_sum).astype(jnp.bfloat16)
    for h in range(heads):
        out_ref[:, h * HEAD_DIM : (h + 1) * HEAD_DIM] = result[h * TOK_DEV : (h + 1) * TOK_DEV]


def attention(query_rows, kv_all, heads):
    columns, blocks = kv_all.shape[:2]
    parts = max(1, columns * TOK_DEV // 512)
    width = heads * HEAD_DIM
    pairs = blocks * TOK_DEV * heads * columns * blocks * TOK_DEV // 2
    return pl.pallas_call(
        functools.partial(attention_kernel, heads, parts),
        grid=(blocks,),
        out_shape=jax.ShapeDtypeStruct((blocks * TOK_DEV, width), jnp.bfloat16),
        in_specs=[
            pl.BlockSpec((TOK_DEV, width), lambda b: (b, 0)),
            pl.BlockSpec(kv_all.shape, lambda b: (0, 0, 0, 0)),
        ],
        out_specs=pl.BlockSpec((TOK_DEV, width), lambda b: (b, 0)),
        compiler_params=pltpu.CompilerParams(vmem_limit_bytes=56 * 1024 * 1024),
        cost_estimate=pl.CostEstimate(
            flops=pairs * 4 * HEAD_DIM * 4,
            bytes_accessed=kv_all.size * 2,
            transcendentals=pairs,
        ),
        name="attention",
    )(query_rows, kv_all)


def middle_kernel(x_ref, v_ref, down_ref, out_ref, total):
    @pl.when(pl.program_id(0) == 0)
    def _():
        total[...] = jnp.zeros_like(total)

    gate = jnp.dot(x_ref[:, :RANK], v_ref[0, 0], preferred_element_type=jnp.float32)
    up = jnp.dot(x_ref[:, RANK:], v_ref[0, 1], preferred_element_type=jnp.float32)
    hidden = (gate / (1.0 + jnp.exp(-gate)) * up).astype(jnp.bfloat16)
    total[...] += jnp.dot(hidden, down_ref[0], preferred_element_type=jnp.float32)

    @pl.when(pl.program_id(0) == pl.num_programs(0) - 1)
    def _():
        out_ref[...] = total[...]


def middle(rank_in, v_gate_up, u_down):
    rows = rank_in.shape[0]
    units = u_down.shape[1]
    tile = min(1024, units)
    return pl.pallas_call(
        middle_kernel,
        grid=(units // tile,),
        out_shape=jax.ShapeDtypeStruct((rows, RANK), jnp.float32),
        in_specs=[
            pl.BlockSpec((rows, 2 * RANK), lambda i: (0, 0)),
            pl.BlockSpec((1, 2, RANK, tile), lambda i: (0, 0, 0, i)),
            pl.BlockSpec((1, tile, RANK), lambda i: (0, i, 0)),
        ],
        out_specs=pl.BlockSpec((rows, RANK), lambda i: (0, 0)),
        scratch_shapes=[pltpu.VMEM((rows, RANK), jnp.float32)],
        compiler_params=pltpu.CompilerParams(vmem_limit_bytes=48 * 1024 * 1024),
        cost_estimate=pl.CostEstimate(
            flops=rows * RANK * units * 6,
            bytes_accessed=units * RANK * 6,
            transcendentals=rows * units,
        ),
        name="middle",
    )(rank_in, v_gate_up, u_down)


def per_device(
    queries,
    keys,
    values,
    residual,
    proj_weight,
    norm_gain,
    router,
    expert_ids,
    u_gate_up,
    v_gate_up,
    u_down,
    v_down,
):
    seq_count = lax.axis_size("seq")
    exp_count = lax.axis_size("exp")
    heads = HEADS // seq_count
    shares = seq_count // KV_HEADS
    kv_send = jnp.concatenate(
        [keys.reshape(TOK_DEV, KV_HEADS, HEAD_DIM), values.reshape(TOK_DEV, KV_HEADS, HEAD_DIM)],
        axis=-1,
    )
    if shares > 1:
        kv_send = jnp.repeat(kv_send, shares, axis=1)
    kv_send = kv_send.reshape(TOK_DEV, seq_count * 2 * HEAD_DIM)
    kv_got = lax.all_to_all(kv_send, "seq", split_axis=1, concat_axis=0, tiled=True)
    kv_all = lax.all_gather(kv_got, "exp", axis=0, tiled=False)
    query_got = lax.all_to_all(queries, "seq", split_axis=1, concat_axis=0, tiled=True)
    query_got, weight_own = lax.optimization_barrier((query_got, proj_weight))
    weight_rows = lax.all_gather(weight_own, "seq", axis=0, tiled=True)
    kv_all = kv_all.reshape(exp_count, seq_count, TOK_DEV, 2 * HEAD_DIM)
    attended = attention(query_got, kv_all, heads)
    attended = lax.all_to_all(attended, "seq", split_axis=0, concat_axis=1, tiled=True)
    half = TOK_DEV // 2
    first_half, weight_rows = lax.optimization_barrier((attended[:half], weight_rows))
    gathered = [
        lax.all_gather(first_half, "exp", axis=0, tiled=True),
        lax.all_gather(attended[half:], "exp", axis=0, tiled=True),
    ]
    updates = []
    for rows in gathered:
        projected = jnp.dot(rows, weight_rows, preferred_element_type=jnp.float32)
        updates.append(
            lax.all_to_all(
                projected.astype(jnp.bfloat16), "exp", split_axis=0, concat_axis=1, tiled=True
            )
        )
    attn_update = jnp.concatenate(updates, axis=0)
    stream = residual.astype(jnp.float32) + attn_update.astype(jnp.float32)
    mean_sq = jnp.mean(stream * stream, axis=-1, keepdims=True)
    normed = (stream * lax.rsqrt(mean_sq + EPS) * norm_gain.astype(jnp.float32)).astype(
        jnp.bfloat16
    )
    logits = jnp.dot(normed, router, preferred_element_type=jnp.float32)
    expert_range = jnp.arange(EXPERTS, dtype=jnp.int32)
    picked = (expert_ids[:, :, None] == expert_range[None, None, :]).astype(jnp.float32)
    chosen = jnp.sum(picked * logits[:, None, :], axis=-1)
    mix_first = jax.nn.sigmoid(chosen[:, 0] - chosen[:, 1])
    mix_second = jax.nn.sigmoid(chosen[:, 1] - chosen[:, 0])
    piece_count = exp_count // EXPERTS
    piece_width = D // piece_count
    flat_ids = expert_ids.reshape(TOK_DEV * 2)
    member = (flat_ids[:, None] == expert_range[None, :]).astype(jnp.int32)
    slot_of = jnp.sum((jnp.cumsum(member, axis=0) - 1) * member, axis=1)
    dest = (flat_ids * CAP + slot_of).reshape(TOK_DEV, 2)
    places = jnp.arange(EXPERTS * CAP, dtype=jnp.int32)
    first_at = dest[:, 0:1] == places[None, :]
    second_at = dest[:, 1:2] == places[None, :]
    select = (first_at | second_at).astype(jnp.bfloat16)
    send_rows = lax.dot_general(
        select, normed, (((0,), (0,)), ((), ())), preferred_element_type=jnp.float32
    ).astype(jnp.bfloat16)
    if piece_count > 1:
        send_rows = send_rows.reshape(EXPERTS, CAP, piece_count, piece_width).transpose(0, 2, 1, 3)
    send_rows = send_rows.reshape(exp_count, CAP, piece_width)
    dispatched = lax.all_to_all(send_rows, "exp", split_axis=0, concat_axis=0, tiled=True)
    expert_rows = dispatched.reshape(exp_count * CAP, piece_width)
    rank_sum = jnp.dot(expert_rows, u_gate_up[0], preferred_element_type=jnp.float32)
    for bit_index in range(piece_count.bit_length() - 1):
        rank_sum = rank_sum + swapped(rank_sum.astype(jnp.bfloat16), "exp", bit_index).astype(
            rank_sum.dtype
        )
    down_sum = middle(rank_sum.astype(jnp.bfloat16), v_gate_up, u_down)
    for bit_index in range(piece_count.bit_length() - 1):
        down_sum = down_sum + swapped(down_sum.astype(jnp.bfloat16), "exp", bit_index).astype(
            down_sum.dtype
        )
    expert_out = jnp.dot(
        down_sum.astype(jnp.bfloat16), v_down[0], preferred_element_type=jnp.float32
    ).astype(jnp.bfloat16)
    returned = lax.all_to_all(
        expert_out.reshape(exp_count, CAP, piece_width),
        "exp",
        split_axis=0,
        concat_axis=0,
        tiled=True,
    )
    if piece_count > 1:
        returned = returned.reshape(EXPERTS, piece_count, CAP, piece_width).transpose(0, 2, 1, 3)
    returned_rows = returned.reshape(EXPERTS * CAP, D)
    mix = mix_first[:, None] * first_at.astype(jnp.float32) + mix_second[
        :, None
    ] * second_at.astype(jnp.float32)
    mix_high = lax.reduce_precision(mix, 8, 7)
    mix_low = (mix - mix_high).astype(jnp.bfloat16)
    mixture = jnp.dot(
        mix_high.astype(jnp.bfloat16), returned_rows, preferred_element_type=jnp.float32
    ) + jnp.dot(mix_low, returned_rows, preferred_element_type=jnp.float32)
    return (stream + mixture).astype(jnp.bfloat16)


def solution(mesh):
    in_specs = (
        P(("seq", "exp"), None),
        P(("seq", "exp"), None),
        P(("seq", "exp"), None),
        P(("seq", "exp"), None),
        P("seq", "exp"),
        P(),
        P(),
        P(("seq", "exp"), None),
        P("exp", None, None),
        P("exp", None, None, None),
        P("exp", None, None),
        P("exp", None, None),
    )
    out_specs = P(("seq", "exp"), None)
    return jax.shard_map(
        per_device, mesh=mesh, in_specs=in_specs, out_specs=out_specs, check_vma=False
    )
```

time: 559 us -> 476 us (0.85)
  waiting for transfers between devices: 275 us -> 232 us
  blocking collectives: 92.1 us -> 134 us
  matrix products: 66.2 us -> 30 us
  starting transfers between devices: 44.3 us -> 12.7 us
  Pallas kernels: 0 us -> 30.1 us
  local copies, waits for them, and re-layouts: 45.2 us -> 21.6 us
  other arithmetic: 18.2 us -> 2 us
    ppermute x20 -> x0, waiting for transfers between devices: 73.4 us -> none  [the longest x8 55.4 us: swapped(): lax.ppermute(x, axis, [(i, i ^ 1 << distance) for i in range(lax.axis_siz...]
    all_gather x2 -> x4, waiting for transfers between devices: 63.2 us -> 124 us  [the longest x1 45.2 us: per_device(): lax.all_gather(first_half, 'exp', axis=0, tiled=True)]
    all_to_all x0 -> x3, blocking collectives: none -> 41 us  [the longest x1 16.8 us: per_device(): lax.all_to_all(attended, 'seq', split_axis=0, concat_axis=1, tiled=True)]
    dot_general x28 -> x5, matrix products: 50.3 us -> 18.3 us  [the longest x2 13.6 us: per_device(): projected = jnp.dot(rows, weight_rows, preferred_element_type=jnp.float32)]
    all_to_all x4 -> x2, waiting for transfers between devices: 50.9 us -> 19.3 us  [per_device(): lax.all_to_all(projected.astype(jnp.bfloat16), 'exp', split_axis=0, conca...]
    pallas_call x0 -> x2, Pallas kernels: none -> 30.1 us  [the longest x1 16.7 us: attention(): pl.pallas_call(functools.partial(attention_kernel, heads, parts), grid=(b...]
    ppermute x20 -> x0, starting transfers between devices: 22.4 us -> none  [the longest x12 12.6 us: passed_along(): return lax.ppermute(value, axis, pairs)]
    gather x4 -> x0, local copies, waits for them, and re-layouts: 20 us -> none  [the longest x2 10 us: per_device(): fetched = jnp.take(returned_rows, fetch_index, axis=0).astype(jnp.float32)]
  transfers between devices with their start and end apart: 27 -> 7, of which waited for: 18 -> 6; matrix products, arithmetic and copies ran while one was open for 6% -> 4% of each run, Pallas kernels for 0% -> 4%
where the time goes in v1:
time: 476 us; the launch traced here: 475 us
  waiting for transfers between devices  232 us (49%)
  blocking collectives  134 us (28%)
  Pallas kernels  30.1 us (6%)
  matrix products  30 us (6%)
  local copies, waits for them, and re-layouts  21.6 us (5%)
  between operations  13.5 us (3%)
  starting transfers between devices  12.7 us (3%)
    all_to_all x1, blocking collectives, per_device(): lax.all_to_all(send_rows, 'exp', split_axis=0, concat_axis=0, tiled=True)  92.8 us
    all_to_all x1, waiting for transfers between devices, per_device(): lax.all_to_all(expert_out.reshape(exp_count, CAP, piece_width), 'exp', sp...  87.8 us
    all_gather x1, waiting for transfers between devices, per_device(): lax.all_gather(first_half, 'exp', axis=0, tiled=True)  45.2 us
    all_gather x1, waiting for transfers between devices, per_device(): lax.all_gather(attended[half:], 'exp', axis=0, tiled=True)  39.9 us
    all_gather x1, waiting for transfers between devices, per_device(): weight_rows = lax.all_gather(weight_own, 'seq', axis=0, tiled=True)  25.1 us
    all_to_all x2, waiting for transfers between devices, per_device(): lax.all_to_all(projected.astype(jnp.bfloat16), 'exp', split_axis=0, conca...  19.3 us
    all_to_all x1, blocking collectives, per_device(): lax.all_to_all(attended, 'seq', split_axis=0, concat_axis=1, tiled=True)  16.8 us
    pallas_call x1, Pallas kernels, attention(): pl.pallas_call(functools.partial(attention_kernel, heads, parts), grid=(b...  16.7 us
  transfers between devices with their start and end apart: 7, of which 6 were waited for; matrix products, arithmetic and copies ran while one was open for 4% of the time, Pallas kernels for 4%

profile of v1, /device:TPU:0, one launch (start us, length us, event | category | flops | bytes accessed | tf_op | source)
XLA Modules:
  0.0 475.3 jit_solution(10489104403388478593)
XLA Ops:
  6.5 1.1 copy.79
  7.6 1.0 copy.80
  8.7 0.1 copy.81
  8.8 10.8 %all_to_all.96 = bf16[128,4,256]{2,0,1:T(8,128)(2,1)} all-to-all(bf16[128,4,256]{2,0,1:T(8,128)(2,1)S(1)} %copy.81), channel_id=1, replica_groups=mesh['seq'=4,'exp'=8] {'seq'}, dimensions={1} | all-to-all | bytes 524288 | tf_op jit(solution)/shard_map/all_to_all | solution.py:162
  19.6 0.0 all-gather.5.cloned.1.call-update
  19.7 0.0 all-gather.7.cloned.1.call-start
  19.7 1.2 copy.95
  20.9 13.4 %all_to_all.97 = bf16[128,4,768]{2,0,1:T(8,128)(2,1)} all-to-all(bf16[128,4,768]{2,0,1:T(8,128)(2,1)S(1)} %bitcast.69), channel_id=1, replica_groups=mesh['seq'=4,'exp'=8] {'seq'}, dimensions={1} | all-to-all | bytes 1572864 | tf_op jit(solution)/shard_map/all_to_all | solution.py:164
  34.3 0.0 all-gather.7.cloned.1.call-update
  34.3 0.0 all-gather.11.cloned.1.call-start
  34.4 14.3 %all-gather.5.cloned.1.call-done = bf16[8,512,256]{2,1,0:T(8,128)(2,1)} async-done(((bf16[1,512,256]{2,1,0:T(8,128)(2,1)}), bf16[8,512,256]{2,1,0:T(8,128)(2,1)}) %all-gather.5.cloned.1.call-update) | async-done | bytes 2097168 | tf_op jit(solution)/shard_map/all_gather | solution.py:163
  48.7 16.7 %attention.1 = bf16[512,768]{1,0:T(8,128)(2,1)} custom-call(bf16[512,768]{1,0:T(8,128)(2,1)} %bitcast.74, bf16[8,4,128,256]{3,2,1,0:T(8,128)(2,1)} %bitcast.78), custom_call_target="tpu_custom_call" | custom-call | flops 12884901888 | bytes 2097152 | tf_op jit(solution)/shard_map/attention/pallas_call | solution.py:78
  65.3 16.8 %all_to_all.98 = bf16[4,128,768]{2,1,0:T(8,128)(2,1)S(1)} all-to-all(bf16[4,128,768]{2,1,0:T(8,128)(2,1)} %bitcast.75), channel_id=1, replica_groups=mesh['seq'=4,'exp'=8] {'seq'}, dimensions={0} | all-to-all | bytes 1572864 | tf_op jit(solution)/shard_map/all_to_all | solution.py:169
  82.2 0.1 slice_bitcast_fusion.1
  82.2 0.8 copy.92
  83.0 0.0 all-gather.11.cloned.1.call-update
  83.0 0.0 all-gather.9.cloned.1.call-start
  83.1 0.8 copy.90
  83.8 25.1 %all-gather.7.cloned.1.call-done = bf16[3072,768]{1,0:T(8,128)(2,1)} async-done(((bf16[768,768]{1,0:T(8,128)(2,1)}), bf16[3072,768]{1,0:T(8,128)(2,1)}) %all-gather.7.cloned.1.call-update) | async-done | bytes 4718608 | tf_op jit(solution)/shard_map/all_gather | solution.py:166
  109.0 0.0 all-gather.9.cloned.1.call-update
  109.0 39.9 %all-gather.11.cloned.1.call-done = bf16[512,3072]{1,0:T(8,128)(2,1)} async-done(((bf16[64,3072]{1,0:T(8,128)(2,1)}), bf16[512,3072]{1,0:T(8,128)(2,1)}) %all-gather.11.cloned.1.call-update) | async-done | bytes 3145744 | tf_op jit(solution)/shard_map/all_gather | solution.py:174
  148.9 6.8 %convolution_convert_fusion.2 = bf16[512,768]{1,0:T(8,128)(2,1)} fusion(bf16[512,3072]{1,0:T(8,128)(2,1)} %all-gather.11.cloned.1.call-done, bf16[3072,768]{1,0:T(8,128)(2,1)} %all-gather.7.cloned.1.call-done), kind=kOutput, calls=%fused_computation.12 | convolution fusion | flops 2416312320 | bytes 8650752 | tf_op jit(solution)/shard_map/dot_general | solution.py:178
  155.7 3.5 all-to-all-start.4
  159.2 0.0 copy-start.10
  159.2 0.0 copy-start.9
  159.2 45.2 %all-gather.9.cloned.1.call-done = bf16[512,3072]{1,0:T(8,128)(2,1)} async-done(((bf16[64,3072]{1,0:T(8,128)(2,1)}), bf16[512,3072]{1,0:T(8,128)(2,1)}) %all-gather.9.cloned.1.call-update) | async-done | bytes 3145744 | tf_op jit(solution)/shard_map/all_gather | solution.py:173
  204.4 6.9 %convolution_convert_fusion.3 = bf16[512,768]{1,0:T(8,128)(2,1)} fusion(bf16[512,3072]{1,0:T(8,128)(2,1)} %all-gather.9.cloned.1.call-done, bf16[3072,768]{1,0:T(8,128)(2,1)} %all-gather.7.cloned.1.call-done), kind=kOutput, calls=%fused_computation.13 | convolution fusion | flops 2416312320 | bytes 8650752 | tf_op jit(solution)/shard_map/dot_general | solution.py:178
  211.3 0.0 all-to-all-done.4
  211.3 4.3 all-to-all-start.3
  215.6 0.1 copy.86
  215.8 0.1 eq.72
  215.9 0.1 eq.68
  216.0 0.0 copy-done.9
  216.1 0.6 reduce-window.6
  216.7 0.2 slice_reduce_fusion
  216.9 0.1 fusion.26
  217.0 0.1 reduce_sum.30
  217.2 0.1 copy.88
  217.2 0.1 copy.93
  217.3 0.0 copy-start.5
  217.3 19.3 %all-to-all-done.3 = bf16[8,64,768]{2,1,0:T(8,128)(2,1)} async-done(((bf16[8,64,768]{2,1,0:T(8,128)(2,1)}), bf16[8,64,768]{2,1,0:T(8,128)(2,1)}, u32[]{:S(2)}, u32[]{:S(2)}) %all-to-all-start.3) | async-done | bytes 786464 | tf_op jit(solution)/shard_map/all_to_all | solution.py:180
  236.6 1.2 copy.91
  237.8 0.6 multiply_reduce_fusion
  238.4 0.6 multiply_convert_fusion
  239.0 0.0 copy-start.3
  239.1 1.1 copy-done.3
  240.2 1.1 convolution_convert_fusion.1
  241.3 3.0 reshape.78
  244.3 92.8 %all_to_all.99 = bf16[8,33,6144]{2,1,0:T(8,128)(2,1)} all-to-all(bf16[8,33,6144]{2,1,0:T(8,128)(2,1)} %reshape.78), channel_id=1, replica_groups=mesh['seq'=4,'exp'=8] {'exp'}, dimensions={0} | all-to-all | bytes 6488064 | tf_op jit(solution)/shard_map/all_to_all | solution.py:212
  337.2 3.3 reshape.79
  340.4 6.6 %fusion.5.x_ref = bf16[264,1024]{1,0:T(8,128)(2,1)S(1)} fusion(bf16[264,6144]{1,0:T(8,128)(2,1)S(1)} %reshape.79, bf16[1,6144,1024]{2,1,0:T(8,128)(2,1)} %param.20), kind=kOutput, calls=%fused_computation.14 | convolution fusion | flops 3322159104 | bytes 16367616 | tf_op jit(solution)/shard_map/dot_general | solution.py:214
  347.0 13.4 %middle.1 = f32[264,512]{1,0:T(8,128)S(1)} custom-call(bf16[264,1024]{1,0:T(8,128)(2,1)S(1)} %fusion.5.x_ref, bf16[1,2,512,8192]{3,2,1,0:T(8,128)(2,1)} %v_ref.1, bf16[1,8192,512]{2,1,0:T(8,128)(2,1)} %down_ref.1), custom_call_target="tpu_custom_call" | custom-call | flops 6643777536 | bytes 25165824 | tf_op jit(solution)/shard_map/middle/pallas_call | solution.py:116
  360.4 4.6 convolution_convert_fusion
  365.1 3.1 reshape.80
  368.1 4.7 all-to-all-start.6
  372.8 0.5 fusion.30
  373.4 87.8 %all-to-all-done.6 = bf16[8,33,6144]{2,1,0:T(8,128)(2,1)} async-done(((bf16[8,33,6144]{2,1,0:T(8,128)(2,1)}), bf16[8,33,6144]{2,1,0:T(8,128)(2,1)}, u32[]{:S(2)}, u32[]{:S(2)}) %all-to-all-start.6) | async-done | bytes 3244064 | tf_op jit(solution)/shard_map/all_to_all | solution.py:227
  461.2 3.3 reshape.81
  464.4 0.0 copy-start.2
  464.5 1.1 fusion.13
  465.6 0.3 copy-done.2
  465.9 0.2 copy-done.6
  466.1 0.2 copy-done.8
  466.3 2.5 fusion.3
  (23 shorter events, 0.2 us)
Async XLA Ops:
  6.5 366.3 %copy-start = (bf16[6144,8]{0,1:T(8,128)(2,1)S(1)}, bf16[6144,8]{0,1:T(8,128)(2,1)}, u32[]{:S(2)}) copy-start(bf16[6144,8]{0,1:T(8,128)(2,1)} %param.18) | copy-start | bytes 294916
  6.5 42.1 %all-gather.5.cloned.1.call-start = ((), (), s32[]{:S(2)}) async-start(), calls=%async_computation.7 | async-start | bytes 2359296 | tf_op jit(solution)/shard_map/all_gather | solution.py:163
  19.7 89.3 %all-gather.7.cloned.1.call-start = ((), (), s32[]{:S(2)}) async-start(), calls=%async_computation.8 | async-start | bytes 5898240 | tf_op jit(solution)/shard_map/all_gather | solution.py:166
  34.3 114.6 %all-gather.11.cloned.1.call-start = ((), (), s32[]{:S(2)}) async-start(), calls=%async_computation.10 | async-start | bytes 3538944 | tf_op jit(solution)/shard_map/all_gather | solution.py:174
  83.0 121.4 %all-gather.9.cloned.1.call-start = ((), (), s32[]{:S(2)}) async-start(), calls=%async_computation.9 | async-start | bytes 3538944 | tf_op jit(solution)/shard_map/all_gather | solution.py:173
  155.7 55.6 %all-to-all-start.4 = ((bf16[8,64,768]{2,1,0:T(8,128)(2,1)}), bf16[8,64,768]{2,1,0:T(8,128)(2,1)S(1)}, u32[]{:S(2)}, u32[]{:S(2)}) async-start(bf16[8,64,768]{2,1,0:T(8,128)(2,1)} %bitcast.11), calls=%async_computation.4 | async-start | bytes 1572864 | tf_op jit(solution)/shard_map/all_to_all | solution.py:180
  159.2 56.4 %copy-start.10 = (s32[128,2]{0,1:T(2,128)S(1)}, s32[128,2]{0,1:T(2,128)}, u32[]{:S(2)}) copy-start(s32[128,2]{0,1:T(2,128)} %param.19) | copy-start | bytes 3076
  159.2 56.8 %copy-start.9 = (bf16[6144]{0:T(1024)(128)(2,1)S(1)}, bf16[6144]{0:T(1024)(128)(2,1)}, u32[]{:S(2)}) copy-start(bf16[6144]{0:T(1024)(128)(2,1)} %param.17) | copy-start | bytes 36868
  211.3 26.5 %copy-start.1 = (bf16[128,6144]{1,0:T(8,128)(2,1)S(1)}, bf16[128,6144]{1,0:T(8,128)(2,1)}, u32[]{:S(2)}) copy-start(bf16[128,6144]{1,0:T(8,128)(2,1)} %param.15) | copy-start | bytes 4718596
  211.3 25.3 %all-to-all-start.3 = ((bf16[8,64,768]{2,1,0:T(8,128)(2,1)}), bf16[8,64,768]{2,1,0:T(8,128)(2,1)}, u32[]{:S(2)}, u32[]{:S(2)}) async-start(bf16[8,64,768]{2,1,0:T(8,128)(2,1)} %bitcast.9), calls=%async_computation.3 | async-start | bytes 1572864 | tf_op jit(solution)/shard_map/all_to_all | solution.py:180
  217.3 21.7 %copy-start.5 = (bf16[8,8,8,768]{3,2,0,1:T(8,128)(2,1)}, bf16[8,8,8,768]{3,2,0,1:T(8,128)(2,1)S(1)}, u32[]{:S(2)}) copy-start(bf16[8,8,8,768]{3,2,0,1:T(8,128)(2,1)S(1)} %copy.93) | copy-start | bytes 2359300
  237.8 1.3 copy-start.7
  239.0 1.1 copy-start.3
  368.1 4.7 copy-start.4
  368.1 93.0 %all-to-all-start.6 = ((bf16[8,33,6144]{2,1,0:T(8,128)(2,1)}), bf16[8,33,6144]{2,1,0:T(8,128)(2,1)}, u32[]{:S(2)}, u32[]{:S(2)}) async-start(bf16[8,33,6144]{2,1,0:T(8,128)(2,1)} %reshape.80), calls=%async_computation.6 | async-start | bytes 7864320 | tf_op jit(solution)/shard_map/all_to_all | solution.py:227
  464.4 1.4 copy-start.2
  464.5 1.6 copy-start.6
  464.5 1.8 copy-start.8
Sparse Core Ops, SparseCore 0:
  19.8 28.8 all-gather.4
  50.5 58.4 all-gather.6
  110.6 38.2 all-gather.10
  150.4 53.9 all-gather.8
